TPU v7x, 32 devices: a whole 2x2x4 slice. The times are simulated.
32 devices in a mesh: grp: 2 (over y), seq: 16 (over z, x, core), head: 1.
Axes of the slice: x: 2, y: 2, z: 4, core: 2. Of those that a mesh axis runs over, the one named last changes fastest.
Arguments:
- queries: bfloat16 [2048, 1, 128], P(('grp', 'seq'), 'head'), parts along dimension 0, may hold values from -6 to 6
- keys: bfloat16 [256, 512, 8, 128], P(('grp', 'seq'), None, 'head'), parts along dimension 0, may hold values from -28 to 28
- values: bfloat16 [256, 512, 8, 128], P(('grp', 'seq'), None, 'head'), parts along dimension 0, may hold values from -6 to 6
- lengths: int32 [32], P('grp'), parts along dimension 0, may hold values from 1 to 4096, 40960 in all
- slot_block: int32 [256], P(('grp', 'seq')), parts along dimension 0, may hold values from 0 to 127, each once
Outputs:
- attended: bfloat16 [2048, 1, 128], P(('grp', 'seq'), 'head'), parts along dimension 0
There are 2 independent parts, one for each index of `grp`. A program takes and returns all parts, laid end to end along the dimension named above; each array names one. Nothing has to cross between parts.
Inputs may be any that keep to these rules, and one draw needn't show every extreme that they name: `slot_block`: each slot holds a different logical block; every block of every sequence has a slot. `lengths`: every sequence has at least one token.
All inputs are finite; a program needn't handle non-finite values.
Results may differ from a plain program's by a relative error of at most 0.0055.
Values may be sent and summed in bfloat16 or wider, within the bound.
A program may use at most 64 MiB of HBM per device.

v0:
```python
import functools
import jax
import jax.numpy as jnp
from jax import lax
from jax.experimental import pallas as pl
from jax.experimental.pallas import tpu as pltpu
from jax.sharding import PartitionSpec as P

LANES = 128
MESH_ID = pl.DeviceIdType.MESH
LOW = -1e30


def spread(tile, start, heads):
    group = tile.shape[0]
    return jnp.concatenate(
        [jnp.broadcast_to(tile[:, start + h : start + h + 1], (group, LANES)) for h in range(heads)],
        axis=0,
    )


def fold(tile, step, op):
    shift = LANES // 2
    while shift >= step:
        tile = op(tile, pltpu.roll(tile, shift, 1))
        shift //= 2
    return tile


def unpack(tile, lane):
    turned = pltpu.roll(tile, LANES // 2, 1)
    low = lane < LANES // 2
    return jnp.where(low, tile, turned), jnp.where(low, turned, tile)


def kernel(
    n, batch, block, kv, factor,
    lengths_hbm, block_hbm, q_hbm, k_hbm, v_hbm, out_ref,
    lengths, slot_block, q_ref, q_all, k_buf, v_buf, parts, peaks, totals,
    acc, stat, acc_in, stat_in, acc2, stat2, acc2_in, stat2_in,
    k_sem, v_sem, own_sem, in_sem, qs_sem, qr_sem, fs_sem, s1_sem, r1_sem, s2_sem, r2_sem, t2_sem, u2_sem,
):
    slots, cols, hd = k_buf.shape
    share = q_ref.shape[0]
    outer = n // 2
    per = n // batch
    heads = per * share
    group = heads // kv
    held = share // group
    me = lax.axis_index("seq")
    mine, inner = me // 2, me % 2
    partner = me + 1 - 2 * inner

    def k_copy(s):
        return pltpu.make_async_copy(k_hbm.at[s], k_buf.at[s], k_sem.at[s])

    def v_copy(s):
        return pltpu.make_async_copy(v_hbm.at[s], v_buf.at[s], v_sem.at[s])

    q_in = pltpu.make_async_copy(q_hbm, q_ref, in_sem.at[0])
    q_in.start()
    peers = [(mine + r) % outer for r in range(1, outer)]
    barrier = pltpu.get_barrier_semaphore()
    pl.semaphore_signal(barrier, inc=1, device_id={"seq": partner}, device_id_type=MESH_ID)
    for o in peers:
        pl.semaphore_signal(barrier, inc=1, device_id={"seq": o * 2 + inner}, device_id_type=MESH_ID)
    len_in = pltpu.make_async_copy(lengths_hbm, lengths, in_sem.at[1])
    block_in = pltpu.make_async_copy(block_hbm, slot_block, in_sem.at[2])
    len_in.start()
    block_in.start()
    own = pltpu.make_async_copy(q_hbm, q_all.at[me], own_sem)
    own.start()
    for s in range(slots):
        k_copy(s).start()
        v_copy(s).start()
    q_in.wait()
    pl.semaphore_wait(barrier, outer)

    def remote(src, dst, ssem, rsem, dev):
        return pltpu.make_async_remote_copy(
            src_ref=src, dst_ref=dst, send_sem=ssem, recv_sem=rsem,
            device_id={"seq": dev}, device_id_type=MESH_ID,
        )

    sends = []
    for r, o in enumerate(peers):
        sends.append(remote(q_ref, q_all.at[me], qs_sem.at[r], qr_sem.at[me], o * 2 + inner))
    sends.append(remote(q_ref, q_all.at[me], qs_sem.at[outer - 1], qr_sem.at[me], partner))
    for c in sends:
        c.start()
    forwards = []
    for r in range(1, outer):
        src = ((mine + outer - r) % outer) * 2 + inner
        remote(q_ref, q_all.at[src], qs_sem.at[0], qr_sem.at[src], partner).wait_recv()
        c = remote(q_all.at[src], q_all.at[src], fs_sem.at[r - 1], qr_sem.at[src], partner)
        c.start()
        forwards.append(c)
    remote(q_ref, q_all.at[partner], qs_sem.at[0], qr_sem.at[partner], partner).wait_recv()
    for r in range(1, outer):
        src = ((mine + outer - r) % outer) * 2 + 1 - inner
        remote(q_ref, q_all.at[src], qs_sem.at[0], qr_sem.at[src], partner).wait_recv()
    for s in range(slots):
        k_copy(s).wait()
        v_copy(s).wait()
    own.wait()
    len_in.wait()
    block_in.wait()

    lane = lax.broadcasted_iota(jnp.int32, (group, LANES), 1)
    chunk = min(cols, 512)
    wide = lax.broadcasted_iota(jnp.int32, (group, chunk), 1)
    picks = [wide % kv == h for h in range(kv)]

    def one_slot(s, carry):
        code = slot_block[s]
        seq = code // (slots * n // batch)
        blk = code % (slots * n // batch)
        limit = (lengths[seq] - blk * block) * kv
        q = q_all[pl.ds(seq * per, per)]
        if per > 1:
            q = q.astype(jnp.float32).reshape(heads, hd).astype(jnp.bfloat16)
        else:
            q = q.reshape(heads, hd)
        scores = []
        top = jnp.full((group, LANES), LOW, jnp.float32)
        for c in range(0, cols, chunk):
            full = lax.dot_general(
                q, k_buf[s, c : c + chunk, :], (((1,), (1,)), ((), ())),
                preferred_element_type=jnp.float32,
            )
            packed = full[:group]
            for h in range(1, kv):
                packed = jnp.where(picks[h], full[h * group : (h + 1) * group], packed)
            packed = jnp.where(wide < limit - c, packed * factor, LOW)
            scores.append(packed)
            for l in range(0, chunk, LANES):
                top = jnp.maximum(top, packed[:, l : l + LANES])
        top = fold(top, kv, jnp.maximum)
        top_wide = jnp.concatenate([top] * (chunk // LANES), axis=1)
        total = jnp.zeros((group, LANES), jnp.float32)
        part = jnp.zeros((heads, hd), jnp.float32)
        for i, c in enumerate(range(0, cols, chunk)):
            weight = jnp.where(wide < limit - c, jnp.exp(scores[i] - top_wide), 0.0)
            weight = weight.astype(jnp.bfloat16).astype(jnp.float32)
            for l in range(0, chunk, LANES):
                total = total + weight[:, l : l + LANES]
            spread_w = jnp.concatenate(
                [jnp.where(picks[h], weight, 0.0) for h in range(kv)], axis=0
            ).astype(jnp.bfloat16)
            part = part + jnp.dot(
                spread_w, v_buf[s, c : c + chunk, :], preferred_element_type=jnp.float32
            )
        parts[s] = part
        peaks[s] = top
        totals[s] = fold(total, kv, jnp.add)
        return carry

    lax.fori_loop(0, slots, one_slot, 0, unroll=4)

    seqs = [slot_block[s] // (slots * n // batch) for s in range(slots)]
    for s in range(slots):
        best = peaks[s]
        for t in range(slots):
            if t != s:
                best = jnp.maximum(best, jnp.where(seqs[t] == seqs[s], peaks[t], LOW))
        scale = jnp.exp(peaks[s] - best)
        totals[s] = totals[s] * scale
        parts[s] = parts[s] * spread(scale, 0, kv)
    low_half = lane < LANES // 2
    for b in range(batch):
        flags = [jnp.where(seqs[s] == b, 1.0, 0.0) for s in range(slots)]
        best = jnp.full((group, LANES), LOW, jnp.float32)
        total = jnp.zeros((group, LANES), jnp.float32)
        out = jnp.zeros((heads, hd), jnp.float32)
        for s in range(slots):
            best = jnp.maximum(best, jnp.where(seqs[s] == b, peaks[s], LOW))
            total = total + flags[s] * totals[s]
            out = out + flags[s] * parts[s]
        for p in range(per):
            j = b * per + p
            turn = (LANES - p * held) % LANES
            tb, tt = best, total
            if turn:
                tb, tt = pltpu.roll(best, turn, 1), pltpu.roll(total, turn, 1)
            stat[j % 2, j // 2] = jnp.where(low_half, tb, tt)
            acc[j % 2, j // 2] = out[p * share : (p + 1) * share]

    c1 = remote(acc.at[1 - inner], acc_in, s1_sem.at[0], r1_sem.at[0], partner)
    c2 = remote(stat.at[1 - inner], stat_in, s1_sem.at[1], r1_sem.at[1], partner)
    c2.start()
    c1.start()
    c2.wait()
    c1.wait()
    last = []
    for r in range(1, outer + 1):
        o = (mine + r) % outer
        ma, la = unpack(stat[inner, o], lane)
        mb, lb = unpack(stat_in[o], lane)
        best = jnp.maximum(ma, mb)
        sa, sb = jnp.exp(ma - best), jnp.exp(mb - best)
        total = sa * la + sb * lb
        both = acc[inner, o] * spread(sa, 0, held) + acc_in[o] * spread(sb, 0, held)
        if r == outer:
            break
        stat2[o] = jnp.where(low_half, best, total)
        acc2[o] = both.astype(jnp.bfloat16)
        dev = o * 2 + inner
        c1 = remote(acc2.at[o], acc2_in.at[mine], s2_sem.at[r - 1], r2_sem.at[mine], dev)
        c2 = remote(stat2.at[o], stat2_in.at[mine], t2_sem.at[r - 1], u2_sem.at[mine], dev)
        c2.start()
        c1.start()
        last += [c1, c2]
    for r in range(1, outer):
        o = (mine + outer - r) % outer
        remote(stat2.at[o], stat2_in.at[o], t2_sem.at[0], u2_sem.at[o], partner).wait_recv()
        remote(acc2.at[o], acc2_in.at[o], s2_sem.at[0], r2_sem.at[o], partner).wait_recv()
        mb, lb = unpack(stat2_in[o], lane)
        new = jnp.maximum(best, mb)
        sa, sb = jnp.exp(best - new), jnp.exp(mb - new)
        total = sa * total + sb * lb
        both = both * spread(sa, 0, held) + acc2_in[o].astype(jnp.float32) * spread(sb, 0, held)
        best = new
    out_ref[...] = (both / spread(total, 0, held)).astype(jnp.bfloat16)
    for c in sends + forwards + last:
        c.wait_send()


def body(queries, keys, values, lengths, slot_block):
    slots, block, kv, hd = keys.shape
    share = queries.shape[0]
    n = lax.axis_size("seq")
    batch = lengths.shape[0]
    heads = n * share // batch
    group = heads // kv
    outer = n // 2
    cols = block * kv
    f32, bf16 = jnp.float32, jnp.bfloat16
    dma = pltpu.SemaphoreType.DMA
    vmem = pl.BlockSpec(memory_space=pltpu.VMEM)
    hbm = pl.BlockSpec(memory_space=pltpu.HBM)
    result = pl.pallas_call(
        functools.partial(kernel, n, batch, block, kv, hd ** (-0.5)),
        out_shape=jax.ShapeDtypeStruct((share, hd), bf16),
        in_specs=[hbm] * 5,
        out_specs=vmem,
        scratch_shapes=[
            pltpu.SMEM(lengths.shape, jnp.int32),
            pltpu.SMEM(slot_block.shape, jnp.int32),
            pltpu.VMEM((share, hd), bf16),
            pltpu.VMEM((n, share, hd), bf16),
            pltpu.VMEM((slots, cols, hd), bf16),
            pltpu.VMEM((slots, cols, hd), bf16),
            pltpu.VMEM((slots, heads, hd), f32),
            pltpu.VMEM((slots, group, LANES), f32),
            pltpu.VMEM((slots, group, LANES), f32),
            pltpu.VMEM((2, outer, share, hd), f32),
            pltpu.VMEM((2, outer, group, LANES), f32),
            pltpu.VMEM((outer, share, hd), f32),
            pltpu.VMEM((outer, group, LANES), f32),
            pltpu.VMEM((outer, share, hd), bf16),
            pltpu.VMEM((outer, group, LANES), f32),
            pltpu.VMEM((outer, share, hd), bf16),
            pltpu.VMEM((outer, group, LANES), f32),
            dma((slots,)), dma((slots,)), dma, dma((3,)),
            dma((outer,)), dma((n,)), dma((outer,)),
            dma((2,)), dma((2,)),
            dma((outer,)), dma((outer,)), dma((outer,)), dma((outer,)),
        ],
        compiler_params=pltpu.CompilerParams(
            collective_id=0, has_side_effects=True, vmem_limit_bytes=67043328
        ),
        name="decode",
    )(
        lengths,
        slot_block,
        queries.reshape(share, hd),
        keys.reshape(slots, cols, hd),
        values.reshape(slots, cols, hd),
    )
    return result.reshape(share, 1, hd)


def solution(mesh):
    placed = (
        P(("grp", "seq"), "head", None),
        P(("grp", "seq"), None, "head", None),
        P(("grp", "seq"), None, "head", None),
        P("grp"),
        P(("grp", "seq")),
    )
    return jax.shard_map(
        body, mesh=mesh, in_specs=placed, out_specs=P(("grp", "seq"), "head", None), check_vma=False
    )
```

profile of v0, /device:TPU:0, one launch (start us, length us, event | category | flops | bytes accessed | tf_op | source)
XLA Modules:
  0.0 30.4 jit_solution(16368293475047405843)
XLA Ops:
  0.0 29.1 %decode.1 = bf16[64,128]{1,0:T(8,128)(2,1)} custom-call(s32[16]{0:T(128)} %lengths_hbm.1, s32[8]{0:T(128)} %block_hbm.1, bf16[64,128]{1,0:T(8,128)(2,1)} %bitcast.7, bf16[8,4096,128]{2,1,0:T(8,128)(2,1)} %bitcast.4, bf16[8,4096,128]{2,1,0:T(8,128)(2,1)} %bitcast.5), custom_call_target="tpu_custom_call" | custom-call | tf_op jit(solution)/shard_map/decode/pallas_call | solution.py:241
  29.1 1.3 %copy.7 = bf16[64,1,128]{2,0,1:T(8,128)(2,1)} copy(bf16[64,1,128]{2,0,1:T(8,128)(2,1)} %bitcast.6) | data formatting | bytes 32768
where the time goes:
time: 30.7 us; the launch traced here: 30.4 us
  Pallas kernels  29.1 us (95%)
  local copies, waits for them, and re-layouts  1.32 us (4%)
    pallas_call x1, Pallas kernels, body(): pl.pallas_call(functools.partial(kernel, n, batch, block, kv, hd ** (-0.5...  29.1 us
    unnamed x1, local copies, waits for them, and re-layouts  1.32 us

commit v1 on v0

v1 whole, which is shorter than its diff:
```python
import functools
import math
import jax
import jax.numpy as jnp
from jax import lax
from jax.experimental import pallas as pl
from jax.experimental.pallas import tpu as pltpu
from jax.sharding import PartitionSpec as P

LANES = 128
MESH_ID = pl.DeviceIdType.MESH
LOW = -1e30
DEAD = -3e38
PAIR = 2


def fold(tile, step, op):
    shift = LANES // 2
    while shift >= step:
        tile = op(tile, pltpu.roll(tile, shift, 1))
        shift //= 2
    return tile


def kernel(
    n, batch, block, kv, factor,
    lengths_hbm, block_hbm, q_hbm, k_hbm, v_hbm, out_ref,
    lengths, slot_block, q_ref, q_all, k_buf, v_buf, base, scores, parts, peaks, totals,
    best_own, best_in, joint, tot_own, tot_in, acc, acc_send, acc_in, stat, acc2, stat2, acc2_in, stat2_in,
    k_sem, v_sem, own_sem, in_sem, qs_sem, qr_sem, fs_sem, bs_sem, br_sem, ps_sem, pr_sem, ts_sem, tr_sem,
    as_sem, ar_sem, ss_sem, sr_sem,
):
    slots = k_buf.shape[0]
    hd = q_ref.shape[1]
    share = q_ref.shape[0]
    outer = n // 2
    per = n // batch
    blocks = slots * n // batch
    heads = per * share
    group = heads // kv
    duo = PAIR * group
    span = PAIR * duo
    groups = heads // span
    rows = share // groups
    quarters = LANES // span
    rep = block * PAIR // quarters
    me = lax.axis_index("seq")
    mine, inner = me // 2, me % 2
    partner = me + 1 - 2 * inner
    k_rows = k_buf.reshape(slots, kv // PAIR, block * PAIR, hd)
    v_rows = v_buf.reshape(slots, kv // PAIR, block * PAIR, hd)

    def k_copy(s, p):
        return pltpu.make_async_copy(k_hbm.at[s, :, p], k_buf.at[s, p], k_sem.at[s, p])

    def v_copy(s, p):
        return pltpu.make_async_copy(v_hbm.at[s, :, p], v_buf.at[s, p], v_sem.at[s, p])

    def remote(src, dst, ssem, rsem, dev):
        return pltpu.make_async_remote_copy(
            src_ref=src, dst_ref=dst, send_sem=ssem, recv_sem=rsem,
            device_id={"seq": dev}, device_id_type=MESH_ID,
        )

    q_in = pltpu.make_async_copy(q_hbm, q_ref, in_sem.at[0])
    q_in.start()
    peers = [(mine + r) % outer for r in range(1, outer)]
    barrier = pltpu.get_barrier_semaphore()
    for o in peers:
        pl.semaphore_signal(barrier, inc=1, device_id={"seq": o * 2 + inner}, device_id_type=MESH_ID)
    pl.semaphore_signal(barrier, inc=1, device_id={"seq": partner}, device_id_type=MESH_ID)
    len_in = pltpu.make_async_copy(lengths_hbm, lengths, in_sem.at[1])
    block_in = pltpu.make_async_copy(block_hbm, slot_block, in_sem.at[2])
    len_in.start()
    block_in.start()
    own = pltpu.make_async_copy(q_hbm, q_all.at[me], own_sem)
    own.start()
    for g in range(groups):
        for s in range(slots):
            for p in range(PAIR):
                k_copy(s, PAIR * g + p).start()
    for g in range(groups):
        for s in range(slots):
            for p in range(PAIR):
                v_copy(s, PAIR * g + p).start()

    row = lax.broadcasted_iota(jnp.int32, (rep, LANES), 0)
    col = lax.broadcasted_iota(jnp.int32, (rep, LANES), 1)
    base[...] = jnp.where(row % PAIR == col // group % PAIR, row, 1 << 24) + col // span * rep
    q_in.wait()
    pl.semaphore_wait(barrier, outer)

    sends = []
    for r, o in enumerate(peers):
        sends.append(remote(q_ref, q_all.at[me], qs_sem.at[r], qr_sem.at[me], o * 2 + inner))
    sends.append(remote(q_ref, q_all.at[me], qs_sem.at[outer - 1], qr_sem.at[me], partner))
    for c in sends:
        c.start()
    for r in range(1, outer):
        src = ((mine + outer - r) % outer) * 2 + inner
        remote(q_ref, q_all.at[src], qs_sem.at[0], qr_sem.at[src], partner).wait_recv()
        c = remote(q_all.at[src], q_all.at[src], fs_sem.at[r - 1], qr_sem.at[src], partner)
        c.start()
        sends.append(c)
    len_in.wait()
    block_in.wait()
    own.wait()
    remote(q_ref, q_all.at[partner], qs_sem.at[0], qr_sem.at[partner], partner).wait_recv()
    for r in range(1, outer):
        src = ((mine + outer - r) % outer) * 2 + 1 - inner
        remote(q_ref, q_all.at[src], qs_sem.at[0], qr_sem.at[src], partner).wait_recv()

    lane = lax.broadcasted_iota(jnp.int32, (batch, LANES), 1)
    which = lax.broadcasted_iota(jnp.int32, (batch, LANES), 0)
    seqs = [slot_block[s] // blocks for s in range(slots)]

    def score(g, s):
        code = slot_block[s]
        seq, blk = code // blocks, code % blocks
        limit = (lengths[seq] - blk * block) * PAIR
        if per > 1:
            q = q_all[pl.ds(seq * per, per)].astype(jnp.float32).reshape(heads, hd).astype(jnp.bfloat16)
        else:
            q = q_all[seq, g * span : (g + 1) * span]
        blank = jnp.zeros((duo, hd), jnp.bfloat16)
        pair = jnp.concatenate(
            [jnp.concatenate([q[:duo], blank], axis=0), jnp.concatenate([blank, q[duo:]], axis=0)], axis=1
        )
        total = jnp.zeros((rep, LANES), jnp.float32)
        for u in range(quarters):
            at = pl.ds(u * rep, rep)
            keys = jnp.concatenate([k_rows[s, PAIR * g, at, :], k_rows[s, PAIR * g + 1, at, :]], axis=1)
            place = [pair if w == u else jnp.zeros_like(pair) for w in range(quarters)]
            total = total + lax.dot_general(
                keys, jnp.concatenate(place, axis=0), (((1,), (1,)), ((), ())),
                preferred_element_type=jnp.float32,
            )
        masked = jnp.where(base[...] < limit, total * factor, DEAD)
        scores[g, s] = masked
        top = jnp.maximum(jnp.max(masked, axis=0, keepdims=True), LOW)
        peaks[g, pl.ds(s, 1), :] = fold(top, span, jnp.maximum)

    def weigh(g, s):
        seq = slot_block[s] // blocks
        weight = jnp.exp2(scores[g, s] - joint[g, pl.ds(seq, 1), :]).astype(jnp.bfloat16)
        total = jnp.sum(weight.astype(jnp.float32), axis=0, keepdims=True)
        totals[g, pl.ds(s, 1), :] = fold(total, span, jnp.add)
        turned = weight.T
        out = jnp.zeros((span, PAIR * hd), jnp.float32)
        for u in range(quarters):
            at = pl.ds(u * rep, rep)
            vals = jnp.concatenate([v_rows[s, PAIR * g, at, :], v_rows[s, PAIR * g + 1, at, :]], axis=1)
            out = out + jnp.dot(
                turned[u * span : (u + 1) * span], vals, preferred_element_type=jnp.float32
            )
        parts[s] = jnp.concatenate([out[:duo, :hd], out[duo:, hd:]], axis=0)

    def loop(step):
        def one(s, carry):
            step(s)
            return carry
        lax.fori_loop(0, slots, one, 0, unroll=4)

    swaps = []
    for g in range(groups):
        for s in range(slots):
            for p in range(PAIR):
                k_copy(s, PAIR * g + p).wait()
        loop(functools.partial(score, g))
        best = jnp.full((batch, LANES), LOW, jnp.float32)
        for s in range(slots):
            best = jnp.maximum(best, jnp.where(which == seqs[s], peaks[g, s : s + 1, :], LOW))
        best_own[g] = best
        c = remote(best_own.at[g], best_in.at[g], bs_sem.at[g], br_sem.at[g], partner)
        c.start()
        swaps.append(c)

    def spread_out(g):
        total = jnp.zeros((batch, LANES), jnp.float32)
        for s in range(slots):
            total = total + jnp.where(which == seqs[s], totals[g, s : s + 1, :], 0.0)
        tot_own[g] = total
        for b in range(batch):
            out = jnp.zeros((span, hd), jnp.float32)
            for s in range(slots):
                out = out + jnp.where(seqs[s] == b, 1.0, 0.0) * parts[s]
            for p in range(per):
                j = b * per + p
                piece = out[p * rows : (p + 1) * rows]
                acc[g, j % 2, j // 2] = piece
                acc_send[g, j % 2, j // 2] = piece.astype(jnp.bfloat16)
        c1 = remote(acc_send.at[g, 1 - inner], acc_in.at[g], ps_sem.at[g], pr_sem.at[g], partner)
        c2 = remote(tot_own.at[g], tot_in.at[g], ts_sem.at[g], tr_sem.at[g], partner)
        c2.start()
        c1.start()
        return [c1, c2]

    def exchange(g):
        total = tot_own[g] + tot_in[g]
        both = jnp.where(lane % (PAIR * span) < span, joint[g], total)
        for j in range(n):
            b, p = j // per, j % per
            line = both[b : b + 1]
            if p:
                line = pltpu.roll(line, LANES - p * rows, 1)
            stat[g, j % 2, j // 2] = line
        made = []
        for r in range(1, outer + 1):
            o = (mine + r) % outer
            whole = (acc[g, inner, o] + acc_in[g, o].astype(jnp.float32)).astype(jnp.bfloat16)
            if r == outer:
                acc2_in[g, o] = whole
                stat2_in[g, o] = stat[g, inner, o]
                break
            acc2[g, o] = whole
            stat2[g, o] = stat[g, inner, o]
            dev = o * 2 + inner
            c1 = remote(acc2.at[g, o], acc2_in.at[g, mine], as_sem.at[g, r - 1], ar_sem.at[g, mine], dev)
            c2 = remote(stat2.at[g, o], stat2_in.at[g, mine], ss_sem.at[g, r - 1], sr_sem.at[g, mine], dev)
            c2.start()
            c1.start()
            made += [c1, c2]
        return made

    last = []
    for g in range(groups):
        swaps[g].wait()
        joint[g] = jnp.maximum(best_own[g], best_in[g])
        for s in range(slots):
            for p in range(PAIR):
                v_copy(s, PAIR * g + p).wait()
        loop(functools.partial(weigh, g))
        gone = spread_out(g)
        for c in gone:
            c.wait()
        last += exchange(g)

    for g in range(groups):
        for r in range(1, outer):
            o = (mine + outer - r) % outer
            remote(stat2.at[g, o], stat2_in.at[g, o], ss_sem.at[g, 0], sr_sem.at[g, o], partner).wait_recv()
            remote(acc2.at[g, o], acc2_in.at[g, o], as_sem.at[g, 0], ar_sem.at[g, o], partner).wait_recv()
        tops = stat2_in[g].reshape(outer, LANES)
        best = jnp.max(tops, axis=0, keepdims=True)
        scale = jnp.exp2(tops - best)
        total = pltpu.roll(tops, LANES - span, 1)
        scale = scale / jnp.sum(scale * total, axis=0, keepdims=True)
        turned = scale.T
        out = jnp.zeros((rows, hd), jnp.float32)
        for o in range(outer):
            out = out + turned[:rows, o : o + 1] * acc2_in[g, o].astype(jnp.float32)
        out_ref[g * rows : (g + 1) * rows] = out.astype(jnp.bfloat16)
    for c in sends + last:
        c.wait_send()


def body(queries, keys, values, lengths, slot_block):
    slots, block, kv, hd = keys.shape
    share = queries.shape[0]
    n = lax.axis_size("seq")
    batch = lengths.shape[0]
    per = n // batch
    heads = per * share
    duo = PAIR * heads // kv
    span = PAIR * duo
    groups = heads // span
    rows = share // groups
    outer = n // 2
    rep = block * PAIR * span // LANES
    pairs = kv // PAIR
    assert groups == 1 or per == 1
    f32, bf16 = jnp.float32, jnp.bfloat16
    dma = pltpu.SemaphoreType.DMA
    vmem = pl.BlockSpec(memory_space=pltpu.VMEM)
    hbm = pl.BlockSpec(memory_space=pltpu.HBM)
    result = pl.pallas_call(
        functools.partial(kernel, n, batch, block, kv, hd ** (-0.5) * math.log2(math.e)),
        out_shape=jax.ShapeDtypeStruct((share, hd), bf16),
        in_specs=[hbm] * 5,
        out_specs=vmem,
        scratch_shapes=[
            pltpu.SMEM(lengths.shape, jnp.int32),
            pltpu.SMEM(slot_block.shape, jnp.int32),
            pltpu.VMEM((share, hd), bf16),
            pltpu.VMEM((n, share, hd), bf16),
            pltpu.VMEM((slots, pairs, block, PAIR, hd), bf16),
            pltpu.VMEM((slots, pairs, block, PAIR, hd), bf16),
            pltpu.VMEM((rep, LANES), jnp.int32),
            pltpu.VMEM((groups, slots, rep, LANES), f32),
            pltpu.VMEM((slots, span, hd), f32),
            pltpu.VMEM((groups, slots, LANES), f32),
            pltpu.VMEM((groups, slots, LANES), f32),
            pltpu.VMEM((groups, batch, LANES), f32),
            pltpu.VMEM((groups, batch, LANES), f32),
            pltpu.VMEM((groups, batch, LANES), f32),
            pltpu.VMEM((groups, batch, LANES), f32),
            pltpu.VMEM((groups, batch, LANES), f32),
            pltpu.VMEM((groups, 2, outer, rows, hd), f32),
            pltpu.VMEM((groups, 2, outer, rows, hd), bf16),
            pltpu.VMEM((groups, outer, rows, hd), bf16),
            pltpu.VMEM((groups, 2, outer, 1, LANES), f32),
            pltpu.VMEM((groups, outer, rows, hd), bf16),
            pltpu.VMEM((groups, outer, 1, LANES), f32),
            pltpu.VMEM((groups, outer, rows, hd), bf16),
            pltpu.VMEM((groups, outer, 1, LANES), f32),
            dma((slots, pairs)), dma((slots, pairs)), dma, dma((3,)),
            dma((outer,)), dma((n,)), dma((outer,)),
            dma((groups,)), dma((groups,)), dma((groups,)), dma((groups,)), dma((groups,)), dma((groups,)),
            dma((groups, outer)), dma((groups, outer)), dma((groups, outer)), dma((groups, outer)),
        ],
        compiler_params=pltpu.CompilerParams(
            collective_id=0, has_side_effects=True, vmem_limit_bytes=67043328
        ),
        name="decode",
    )(
        lengths,
        slot_block,
        queries.reshape(share, hd),
        keys.reshape(slots, block, pairs, PAIR, hd),
        values.reshape(slots, block, pairs, PAIR, hd),
    )
    return result.reshape(share, 1, hd)


def solution(mesh):
    placed = (
        P(("grp", "seq"), "head", None),
        P(("grp", "seq"), None, "head", None),
        P(("grp", "seq"), None, "head", None),
        P("grp"),
        P(("grp", "seq")),
    )
    return jax.shard_map(
        body, mesh=mesh, in_specs=placed, out_specs=P(("grp", "seq"), "head", None), check_vma=False
    )
```

time: 30.7 us -> 32.3 us (1.052)
  Pallas kernels: 29.1 us -> 30.6 us
    pallas_call x1, Pallas kernels: 29.1 us -> 30.6 us  [body(): pl.pallas_call(functools.partial(kernel, n, batch, block, kv, hd ** (-0.5...]
where the time goes in v1:
time: 32.3 us; the launch traced here: 32 us
  Pallas kernels  30.6 us (95%)
  local copies, waits for them, and re-layouts  1.32 us (4%)
    pallas_call x1, Pallas kernels, body(): pl.pallas_call(functools.partial(kernel, n, batch, block, kv, hd ** (-0.5...  30.6 us
    unnamed x1, local copies, waits for them, and re-layouts  1.32 us

profile of v1, /device:TPU:0, one launch (start us, length us, event | category | flops | bytes accessed | tf_op | source)
XLA Modules:
  0.0 32.0 jit_solution(7214344122514816343)
XLA Ops:
  0.0 30.6 %decode.1 = bf16[64,128]{1,0:T(8,128)(2,1)} custom-call(s32[16]{0:T(128)} %lengths_hbm.1, s32[8]{0:T(128)} %block_hbm.1, bf16[64,128]{1,0:T(8,128)(2,1)} %bitcast.7, bf16[8,512,4,2,128]{4,3,2,1,0:T(2,128)(2,1)} %bitcast.4, bf16[8,512,4,2,128]{4,3,2,1,0:T(2,128)(2,1)} %bitcast.5), custom_call_target="tpu_custom_call" | custom-call | tf_op jit(solution)/shard_map/decode/pallas_call | solution.py:276
  30.6 1.3 %copy.7 = bf16[64,1,128]{2,0,1:T(8,128)(2,1)} copy(bf16[64,1,128]{2,0,1:T(8,128)(2,1)} %bitcast.6) | data formatting | bytes 32768

commit v2 on v0

v2 whole, which is shorter than its diff:
```python
import functools
import math
import jax
import jax.numpy as jnp
from jax import lax
from jax.experimental import pallas as pl
from jax.experimental.pallas import tpu as pltpu
from jax.sharding import PartitionSpec as P

LANES = 128
MESH_ID = pl.DeviceIdType.MESH
LOW = -1e30
DEAD = -3e38


def fold(tile, step, op):
    shift = LANES // 2
    while shift >= step:
        tile = op(tile, pltpu.roll(tile, shift, 1))
        shift //= 2
    return tile


def spread(tile, start, heads):
    group = tile.shape[0]
    return jnp.concatenate(
        [jnp.broadcast_to(tile[:, start + h : start + h + 1], (group, LANES)) for h in range(heads)],
        axis=0,
    )


def unpack(tile, lane):
    turned = pltpu.roll(tile, LANES // 2, 1)
    low = lane < LANES // 2
    return jnp.where(low, tile, turned), jnp.where(low, turned, tile)


def kernel(
    n, batch, block, kv, factor,
    lengths_hbm, block_hbm, q_hbm, k_hbm, v_hbm, out_ref,
    lengths, slot_block, final, q_ref, q_all, k_buf, v_buf, scores, sums, peaks, totals,
    best_own, best_in, tot_own, tot_in, acc_send, acc_in, acc2, stat2, acc2_in, stat2_in,
    k_sem, v_sem, own_sem, in_sem, qs_sem, qr_sem, fs_sem, swap_sem, as_sem, ar_sem, ss_sem, sr_sem,
):
    slots, cols, hd = k_buf.shape
    share = q_ref.shape[0]
    outer = n // 2
    per = n // batch
    blocks = slots * n // batch
    heads = per * share
    group = heads // kv
    held = share // group
    half = cols // 2
    me = lax.axis_index("seq")
    mine, inner = me // 2, me % 2
    partner = me + 1 - 2 * inner

    def k_copy(s):
        return pltpu.make_async_copy(k_hbm.at[s], k_buf.at[s], k_sem.at[s])

    def v_copy(s):
        return pltpu.make_async_copy(v_hbm.at[s], v_buf.at[s], v_sem.at[s])

    def remote(src, dst, ssem, rsem, dev):
        return pltpu.make_async_remote_copy(
            src_ref=src, dst_ref=dst, send_sem=ssem, recv_sem=rsem,
            device_id={"seq": dev}, device_id_type=MESH_ID,
        )

    q_in = pltpu.make_async_copy(q_hbm, q_ref, in_sem.at[0])
    q_in.start()
    peers = [(mine + r) % outer for r in range(1, outer)]
    barrier = pltpu.get_barrier_semaphore()
    for o in peers:
        pl.semaphore_signal(barrier, inc=1, device_id={"seq": o * 2 + inner}, device_id_type=MESH_ID)
    pl.semaphore_signal(barrier, inc=1, device_id={"seq": partner}, device_id_type=MESH_ID)
    len_in = pltpu.make_async_copy(lengths_hbm, lengths, in_sem.at[1])
    block_in = pltpu.make_async_copy(block_hbm, slot_block, in_sem.at[2])
    len_in.start()
    block_in.start()
    own = pltpu.make_async_copy(q_hbm, q_all.at[me], own_sem)
    own.start()
    for s in range(slots):
        k_copy(s).start()
    for s in range(slots):
        v_copy(s).start()
    sums[...] = jnp.zeros_like(sums)
    len_in.wait()
    block_in.wait()
    seqs = [slot_block[s] // blocks for s in range(slots)]
    before = []
    for s in range(slots):
        prev = slots
        for t in range(s):
            prev = jnp.where(seqs[t] == seqs[s], t, prev)
        before.append(prev)
    for b in range(batch):
        last = slots
        for s in range(slots):
            last = jnp.where(seqs[s] == b, s, last)
        final[b] = last
    q_in.wait()
    pl.semaphore_wait(barrier, outer)

    sends = []
    for r, o in enumerate(peers):
        sends.append(remote(q_ref, q_all.at[me], qs_sem.at[r], qr_sem.at[me], o * 2 + inner))
    sends.append(remote(q_ref, q_all.at[me], qs_sem.at[outer - 1], qr_sem.at[me], partner))
    for c in sends:
        c.start()
    for r in range(1, outer):
        src = ((mine + outer - r) % outer) * 2 + inner
        remote(q_ref, q_all.at[src], qs_sem.at[0], qr_sem.at[src], partner).wait_recv()
        c = remote(q_all.at[src], q_all.at[src], fs_sem.at[r - 1], qr_sem.at[src], partner)
        c.start()
        sends.append(c)
    own.wait()
    remote(q_ref, q_all.at[partner], qs_sem.at[0], qr_sem.at[partner], partner).wait_recv()
    for r in range(1, outer):
        src = ((mine + outer - r) % outer) * 2 + 1 - inner
        remote(q_ref, q_all.at[src], qs_sem.at[0], qr_sem.at[src], partner).wait_recv()

    lane = lax.broadcasted_iota(jnp.int32, (group, LANES), 1)
    home = lane // kv
    chunk = min(half, 512)
    wide = lax.broadcasted_iota(jnp.int32, (group, chunk), 1)
    picks = [wide % kv == h for h in range(kv)]

    def score(s):
        code = slot_block[s]
        seq, blk = code // blocks, code % blocks
        limit = (lengths[seq] - blk * block) * kv
        q = q_all[pl.ds(seq * per, per)]
        if per > 1:
            q = q.astype(jnp.float32).reshape(heads, hd).astype(jnp.bfloat16)
        else:
            q = q.reshape(heads, hd)
        blank = jnp.zeros_like(q)
        both = jnp.concatenate(
            [jnp.concatenate([q, blank], axis=0), jnp.concatenate([blank, q], axis=0)], axis=1
        )
        top = jnp.full((group, LANES), LOW, jnp.float32)
        for c in range(0, half, chunk):
            keys = jnp.concatenate(
                [k_buf[s, c : c + chunk, :], k_buf[s, half + c : half + c + chunk, :]], axis=1
            )
            full = lax.dot_general(
                both, keys, (((1,), (1,)), ((), ())), preferred_element_type=jnp.float32
            )
            for x, at in ((0, c), (heads, half + c)):
                packed = full[x : x + group]
                for h in range(1, kv):
                    packed = jnp.where(picks[h], full[x + h * group : x + (h + 1) * group], packed)
                packed = jnp.where(wide < limit - at, packed * factor, DEAD)
                scores[s, :, at : at + chunk] = packed
                for l in range(0, chunk, LANES):
                    top = jnp.maximum(top, packed[:, l : l + LANES])
        peaks[s] = fold(top, kv, jnp.maximum)

    def weigh(s):
        top = jnp.concatenate([peaks[s]] * (chunk // LANES), axis=1)
        total = jnp.zeros((group, LANES), jnp.float32)
        out = jnp.zeros((2 * heads, 2 * hd), jnp.float32)
        for c in range(0, half, chunk):
            rows = []
            for at in (c, half + c):
                weight = jnp.exp2(scores[s, :, at : at + chunk] - top).astype(jnp.bfloat16)
                weight = weight.astype(jnp.float32)
                for l in range(0, chunk, LANES):
                    total = total + weight[:, l : l + LANES]
                rows += [jnp.where(picks[h], weight, 0.0) for h in range(kv)]
            vals = jnp.concatenate(
                [v_buf[s, c : c + chunk, :], v_buf[s, half + c : half + c + chunk, :]], axis=1
            )
            out = out + jnp.dot(
                jnp.concatenate(rows, axis=0).astype(jnp.bfloat16), vals,
                preferred_element_type=jnp.float32,
            )
        sums[s] = out[:heads, :hd] + out[heads:, hd:]
        totals[s] = fold(total, kv, jnp.add)

    def loop(step):
        def one(s, carry):
            step(s)
            return carry
        lax.fori_loop(0, slots, one, 0, unroll=4)

    for s in range(slots):
        k_copy(s).wait()
    loop(score)
    best = jnp.full((group, LANES), LOW, jnp.float32)
    for s in range(slots):
        best = jnp.maximum(best, jnp.where(home == seqs[s], peaks[s], LOW))
    best_own[...] = best
    swap = remote(best_own, best_in, swap_sem.at[0], swap_sem.at[1], partner)
    swap.start()
    for s in range(slots):
        v_copy(s).wait()
    loop(weigh)
    swap.wait()
    best = jnp.maximum(best_own[...], best_in[...])
    total = jnp.zeros((group, LANES), jnp.float32)
    for s in range(slots):
        ours = fold(jnp.where(home == seqs[s], best, LOW), kv, jnp.maximum)
        scale = jnp.exp2(peaks[s] - ours)
        total = total + jnp.where(home == seqs[s], totals[s] * scale, 0.0)
        sums[s] = sums[s] * spread(scale, 0, kv) + sums[before[s]]

    def piece(o, core):
        j = o * 2 + core
        if per == 1:
            return sums[final[j]]
        return sums[final[j // per], pl.ds(pl.multiple_of(j % per * share, share), share), :]

    tot_own[...] = total
    for o in range(outer):
        acc_send[o] = piece(o, 1 - inner).astype(jnp.bfloat16)
    c1 = remote(acc_send, acc_in, swap_sem.at[2], swap_sem.at[3], partner)
    c2 = remote(tot_own, tot_in, swap_sem.at[4], swap_sem.at[5], partner)
    c2.start()
    c1.start()
    c2.wait()
    total = tot_own[...] + tot_in[...]
    stats = []
    for r in range(1, outer + 1):
        o = (mine + r) % outer
        j = o * 2 + inner
        tb = fold(jnp.where(home == j // per, best, LOW), kv, jnp.maximum)
        tt = fold(jnp.where(home == j // per, total, 0.0), kv, jnp.add)
        if per > 1:
            turn = (LANES - j % per * held) % LANES
            tb, tt = pltpu.roll(tb, turn, 1), pltpu.roll(tt, turn, 1)
        stats.append(jnp.where(lane < LANES // 2, tb, tt))
    c1.wait()
    last = []
    for r in range(1, outer + 1):
        o = (mine + r) % outer
        both = (piece(o, inner) + acc_in[o].astype(jnp.float32)).astype(jnp.bfloat16)
        if r == outer:
            acc2_in[o] = both
            stat2_in[o] = stats[r - 1]
            break
        acc2[o] = both
        stat2[o] = stats[r - 1]
        dev = o * 2 + inner
        c1 = remote(acc2.at[o], acc2_in.at[mine], as_sem.at[r - 1], ar_sem.at[mine], dev)
        c2 = remote(stat2.at[o], stat2_in.at[mine], ss_sem.at[r - 1], sr_sem.at[mine], dev)
        c2.start()
        c1.start()
        last += [c1, c2]
    for r in range(1, outer):
        o = (mine + outer - r) % outer
        remote(stat2.at[o], stat2_in.at[o], ss_sem.at[0], sr_sem.at[o], partner).wait_recv()
        remote(acc2.at[o], acc2_in.at[o], as_sem.at[0], ar_sem.at[o], partner).wait_recv()
    pairs = [unpack(stat2_in[o], lane) for o in range(outer)]
    best = pairs[0][0]
    for top, _ in pairs[1:]:
        best = jnp.maximum(best, top)
    scales = [jnp.exp2(top - best) for top, _ in pairs]
    total = scales[0] * pairs[0][1]
    for o in range(1, outer):
        total = total + scales[o] * pairs[o][1]
    out = jnp.zeros((share, hd), jnp.float32)
    for o in range(outer):
        out = out + spread(scales[o] / total, 0, held) * acc2_in[o].astype(jnp.float32)
    out_ref[...] = out.astype(jnp.bfloat16)
    for c in sends + last:
        c.wait_send()


def body(queries, keys, values, lengths, slot_block):
    slots, block, kv, hd = keys.shape
    share = queries.shape[0]
    n = lax.axis_size("seq")
    batch = lengths.shape[0]
    heads = n * share // batch
    group = heads // kv
    outer = n // 2
    cols = block * kv
    assert batch * kv <= LANES
    f32, bf16 = jnp.float32, jnp.bfloat16
    dma = pltpu.SemaphoreType.DMA
    vmem = pl.BlockSpec(memory_space=pltpu.VMEM)
    hbm = pl.BlockSpec(memory_space=pltpu.HBM)
    tile = (group, LANES)
    result = pl.pallas_call(
        functools.partial(kernel, n, batch, block, kv, hd ** (-0.5) * math.log2(math.e)),
        out_shape=jax.ShapeDtypeStruct((share, hd), bf16),
        in_specs=[hbm] * 5,
        out_specs=vmem,
        scratch_shapes=[
            pltpu.SMEM(lengths.shape, jnp.int32),
            pltpu.SMEM(slot_block.shape, jnp.int32),
            pltpu.SMEM((batch,), jnp.int32),
            pltpu.VMEM((share, hd), bf16),
            pltpu.VMEM((n, share, hd), bf16),
            pltpu.VMEM((slots, cols, hd), bf16),
            pltpu.VMEM((slots, cols, hd), bf16),
            pltpu.VMEM((slots, group, cols), f32),
            pltpu.VMEM((slots + 1, heads, hd), f32),
            pltpu.VMEM((slots, *tile), f32),
            pltpu.VMEM((slots, *tile), f32),
            pltpu.VMEM(tile, f32),
            pltpu.VMEM(tile, f32),
            pltpu.VMEM(tile, f32),
            pltpu.VMEM(tile, f32),
            pltpu.VMEM((outer, share, hd), bf16),
            pltpu.VMEM((outer, share, hd), bf16),
            pltpu.VMEM((outer, share, hd), bf16),
            pltpu.VMEM((outer, *tile), f32),
            pltpu.VMEM((outer, share, hd), bf16),
            pltpu.VMEM((outer, *tile), f32),
            dma((slots,)), dma((slots,)), dma, dma((3,)),
            dma((outer,)), dma((n,)), dma((outer,)), dma((6,)),
            dma((outer,)), dma((outer,)), dma((outer,)), dma((outer,)),
        ],
        compiler_params=pltpu.CompilerParams(
            collective_id=0, has_side_effects=True, vmem_limit_bytes=67043328
        ),
        name="decode",
    )(
        lengths,
        slot_block,
        queries.reshape(share, hd),
        keys.reshape(slots, cols, hd),
        values.reshape(slots, cols, hd),
    )
    return result.reshape(share, 1, hd)


def solution(mesh):
    placed = (
        P(("grp", "seq"), "head", None),
        P(("grp", "seq"), None, "head", None),
        P(("grp", "seq"), None, "head", None),
        P("grp"),
        P(("grp", "seq")),
    )
    return jax.shard_map(
        body, mesh=mesh, in_specs=placed, out_specs=P(("grp", "seq"), "head", None), check_vma=False
    )
```

time: 30.7 us -> 26.6 us (0.87)
  Pallas kernels: 29.1 us -> 25 us
    pallas_call x1, Pallas kernels: 29.1 us -> 25 us  [body(): pl.pallas_call(functools.partial(kernel, n, batch, block, kv, hd ** (-0.5...]
where the time goes in v2:
time: 26.6 us; the launch traced here: 26.4 us
  Pallas kernels  25 us (94%)
  local copies, waits for them, and re-layouts  1.32 us (5%)
    pallas_call x1, Pallas kernels, body(): pl.pallas_call(functools.partial(kernel, n, batch, block, kv, hd ** (-0.5...  25 us
    unnamed x1, local copies, waits for them, and re-layouts  1.32 us

profile of v2, /device:TPU:0, one launch (start us, length us, event | category | flops | bytes accessed | tf_op | source)
XLA Modules:
  0.0 26.4 jit_solution(11521519206558311302)
XLA Ops:
  0.0 25.0 %decode.1 = bf16[64,128]{1,0:T(8,128)(2,1)} custom-call(s32[16]{0:T(128)} %lengths_hbm.1, s32[8]{0:T(128)} %block_hbm.1, bf16[64,128]{1,0:T(8,128)(2,1)} %bitcast.7, bf16[8,4096,128]{2,1,0:T(8,128)(2,1)} %bitcast.4, bf16[8,4096,128]{2,1,0:T(8,128)(2,1)} %bitcast.5), custom_call_target="tpu_custom_call" | custom-call | tf_op jit(solution)/shard_map/decode/pallas_call | solution.py:286
  25.0 1.3 %copy.7 = bf16[64,1,128]{2,0,1:T(8,128)(2,1)} copy(bf16[64,1,128]{2,0,1:T(8,128)(2,1)} %bitcast.6) | data formatting | bytes 32768

commit v3 on v2

--- a/solution.py
+++ b/solution.py
@@ -29,18 +29,12 @@
     )
 
 
-def unpack(tile, lane):
-    turned = pltpu.roll(tile, LANES // 2, 1)
-    low = lane < LANES // 2
-    return jnp.where(low, tile, turned), jnp.where(low, turned, tile)
-
-
 def kernel(
     n, batch, block, kv, factor,
     lengths_hbm, block_hbm, q_hbm, k_hbm, v_hbm, out_ref,
-    lengths, slot_block, final, q_ref, q_all, k_buf, v_buf, scores, sums, peaks, totals,
-    best_own, best_in, tot_own, tot_in, acc_send, acc_in, acc2, stat2, acc2_in, stat2_in,
-    k_sem, v_sem, own_sem, in_sem, qs_sem, qr_sem, fs_sem, swap_sem, as_sem, ar_sem, ss_sem, sr_sem,
+    lengths, slot_block, final, q_ref, q_all, k_buf, k_turn, v_buf, scores, sums, peaks, totals,
+    best_own, best_in, tot_own, tot_in, acc_send, acc_in, mail, mail_in,
+    k_sem, v_sem, own_sem, in_sem, qs_sem, qr_sem, fs_sem, swap_sem, as_sem, ar_sem,
 ):
     slots, cols, hd = k_buf.shape
     share = q_ref.shape[0]
@@ -82,8 +76,6 @@
     own.start()
     for s in range(slots):
         k_copy(s).start()
-    for s in range(slots):
-        v_copy(s).start()
     sums[...] = jnp.zeros_like(sums)
     len_in.wait()
     block_in.wait()
@@ -100,6 +92,20 @@
             last = jnp.where(seqs[s] == b, s, last)
         final[b] = last
     q_in.wait()
+    chunk = min(half, 512)
+
+    def turn_keys():
+        def one(s, carry):
+            k_copy(s).wait()
+            v_copy(s).start()
+            for c in range(0, half, chunk):
+                k_turn[s, :hd, c : c + chunk] = k_buf[s, c : c + chunk, :].T
+                k_turn[s, hd:, c : c + chunk] = k_buf[s, half + c : half + c + chunk, :].T
+            return carry
+        lax.fori_loop(0, slots, one, 0)
+
+    early = mine < outer // 2
+    pl.when(early)(turn_keys)
     pl.semaphore_wait(barrier, outer)
 
     sends = []
@@ -108,6 +114,7 @@
     sends.append(remote(q_ref, q_all.at[me], qs_sem.at[outer - 1], qr_sem.at[me], partner))
     for c in sends:
         c.start()
+    pl.when(jnp.logical_not(early))(turn_keys)
     for r in range(1, outer):
         src = ((mine + outer - r) % outer) * 2 + inner
         remote(q_ref, q_all.at[src], qs_sem.at[0], qr_sem.at[src], partner).wait_recv()
@@ -122,7 +129,6 @@
 
     lane = lax.broadcasted_iota(jnp.int32, (group, LANES), 1)
     home = lane // kv
-    chunk = min(half, 512)
     wide = lax.broadcasted_iota(jnp.int32, (group, chunk), 1)
     picks = [wide % kv == h for h in range(kv)]
 
@@ -141,12 +147,7 @@
         )
         top = jnp.full((group, LANES), LOW, jnp.float32)
         for c in range(0, half, chunk):
-            keys = jnp.concatenate(
-                [k_buf[s, c : c + chunk, :], k_buf[s, half + c : half + c + chunk, :]], axis=1
-            )
-            full = lax.dot_general(
-                both, keys, (((1,), (1,)), ((), ())), preferred_element_type=jnp.float32
-            )
+            full = jnp.dot(both, k_turn[s, :, c : c + chunk], preferred_element_type=jnp.float32)
             for x, at in ((0, c), (heads, half + c)):
                 packed = full[x : x + group]
                 for h in range(1, kv):
@@ -183,10 +184,8 @@
         def one(s, carry):
             step(s)
             return carry
-        lax.fori_loop(0, slots, one, 0, unroll=4)
-
-    for s in range(slots):
-        k_copy(s).wait()
+        lax.fori_loop(0, slots, one, 0, unroll=True)
+
     loop(score)
     best = jnp.full((group, LANES), LOW, jnp.float32)
     for s in range(slots):
@@ -212,6 +211,8 @@
             return sums[final[j]]
         return sums[final[j // per], pl.ds(pl.multiple_of(j % per * share, share), share), :]
 
+    sub = lax.broadcasted_iota(jnp.int32, (group, LANES), 0)
+    diagonal = lane % (LANES // 2) // kv == sub
     tot_own[...] = total
     for o in range(outer):
         acc_send[o] = piece(o, 1 - inner).astype(jnp.bfloat16)
@@ -230,39 +231,43 @@
         if per > 1:
             turn = (LANES - j % per * held) % LANES
             tb, tt = pltpu.roll(tb, turn, 1), pltpu.roll(tt, turn, 1)
-        stats.append(jnp.where(lane < LANES // 2, tb, tt))
+        mix = jnp.where(diagonal, jnp.where(lane < LANES // 2, tb, tt), 0.0)
+        line = jnp.sum(mix, axis=0, keepdims=True)
+        first = line.astype(jnp.bfloat16).astype(jnp.float32)
+        second = (line - first).astype(jnp.bfloat16).astype(jnp.float32)
+        third = line - first - second
+        stats.append(jnp.where(sub == 0, first, jnp.where(sub == 1, second, third)).astype(jnp.bfloat16))
     c1.wait()
     last = []
     for r in range(1, outer + 1):
         o = (mine + r) % outer
         both = (piece(o, inner) + acc_in[o].astype(jnp.float32)).astype(jnp.bfloat16)
-        if r == outer:
-            acc2_in[o] = both
-            stat2_in[o] = stats[r - 1]
-            break
-        acc2[o] = both
-        stat2[o] = stats[r - 1]
-        dev = o * 2 + inner
-        c1 = remote(acc2.at[o], acc2_in.at[mine], as_sem.at[r - 1], ar_sem.at[mine], dev)
-        c2 = remote(stat2.at[o], stat2_in.at[mine], ss_sem.at[r - 1], sr_sem.at[mine], dev)
-        c2.start()
-        c1.start()
-        last += [c1, c2]
+        into = mail_in if r == outer else mail
+        into[o, :share] = both
+        into[o, share:] = stats[r - 1]
+        if r < outer:
+            c = remote(mail.at[o], mail_in.at[mine], as_sem.at[r - 1], ar_sem.at[mine], o * 2 + inner)
+            c.start()
+            last.append(c)
     for r in range(1, outer):
         o = (mine + outer - r) % outer
-        remote(stat2.at[o], stat2_in.at[o], ss_sem.at[0], sr_sem.at[o], partner).wait_recv()
-        remote(acc2.at[o], acc2_in.at[o], as_sem.at[0], ar_sem.at[o], partner).wait_recv()
-    pairs = [unpack(stat2_in[o], lane) for o in range(outer)]
-    best = pairs[0][0]
-    for top, _ in pairs[1:]:
-        best = jnp.maximum(best, top)
-    scales = [jnp.exp2(top - best) for top, _ in pairs]
-    total = scales[0] * pairs[0][1]
-    for o in range(1, outer):
-        total = total + scales[o] * pairs[o][1]
+        remote(mail.at[o], mail_in.at[o], as_sem.at[0], ar_sem.at[o], partner).wait_recv()
+    tops = []
+    for o in range(outer):
+        lines = mail_in[o, share:].astype(jnp.float32)
+        line = lines[0:1] + lines[1:2] + lines[2:3]
+        tile = jnp.where(diagonal, line, 0.0)
+        step = kv
+        while step < LANES // 2:
+            tile = tile + pltpu.roll(tile, step, 1)
+            step *= 2
+        tops.append(tile)
+    best = functools.reduce(jnp.maximum, tops)
+    scales = [jnp.exp2(top - best) for top in tops]
+    total = sum(scale * pltpu.roll(top, LANES // 2, 1) for scale, top in zip(scales, tops))
     out = jnp.zeros((share, hd), jnp.float32)
     for o in range(outer):
-        out = out + spread(scales[o] / total, 0, held) * acc2_in[o].astype(jnp.float32)
+        out = out + spread(scales[o] / total, LANES // 2 - kv, held) * mail_in[o, :share].astype(jnp.float32)
     out_ref[...] = out.astype(jnp.bfloat16)
     for c in sends + last:
         c.wait_send()
@@ -285,7 +290,7 @@
     tile = (group, LANES)
     result = pl.pallas_call(
         functools.partial(kernel, n, batch, block, kv, hd ** (-0.5) * math.log2(math.e)),
-        out_shape=jax.ShapeDtypeStruct((share, hd), bf16),
+        out_shape=pltpu.VMEM((share, hd), bf16),
         in_specs=[hbm] * 5,
         out_specs=vmem,
         scratch_shapes=[
@@ -295,6 +300,7 @@
             pltpu.VMEM((share, hd), bf16),
             pltpu.VMEM((n, share, hd), bf16),
             pltpu.VMEM((slots, cols, hd), bf16),
+            pltpu.VMEM((slots, 2 * hd, cols // 2), bf16),
             pltpu.VMEM((slots, cols, hd), bf16),
             pltpu.VMEM((slots, group, cols), f32),
             pltpu.VMEM((slots + 1, heads, hd), f32),
@@ -306,16 +312,14 @@
             pltpu.VMEM(tile, f32),
             pltpu.VMEM((outer, share, hd), bf16),
             pltpu.VMEM((outer, share, hd), bf16),
-            pltpu.VMEM((outer, share, hd), bf16),
-            pltpu.VMEM((outer, *tile), f32),
-            pltpu.VMEM((outer, share, hd), bf16),
-            pltpu.VMEM((outer, *tile), f32),
+            pltpu.VMEM((outer, share + group, hd), bf16),
+            pltpu.VMEM((outer, share + group, hd), bf16),
             dma((slots,)), dma((slots,)), dma, dma((3,)),
             dma((outer,)), dma((n,)), dma((outer,)), dma((6,)),
-            dma((outer,)), dma((outer,)), dma((outer,)), dma((outer,)),
+            dma((outer,)), dma((outer,)),
         ],
         compiler_params=pltpu.CompilerParams(
-            collective_id=0, has_side_effects=True, vmem_limit_bytes=67043328
+            collective_id=0, has_side_effects=True, vmem_limit_bytes=67043328 - max(share * hd * 2, 2**14)
         ),
         name="decode",
     )(

time: 26.6 us -> 23.2 us (0.87)
  Pallas kernels: 25 us -> 22.4 us
  local copies, waits for them, and re-layouts: 1.32 us -> 0.61 us
    pallas_call x1, Pallas kernels: 25 us -> 22.4 us  [body(): pl.pallas_call(functools.partial(kernel, n, batch, block, kv, hd ** (-0.5...]
    unnamed x1, local copies, waits for them, and re-layouts: 1.32 us -> 0.61 us
where the time goes in v3:
time: 23.2 us; the launch traced here: 23.1 us
  Pallas kernels  22.4 us (97%)
  local copies, waits for them, and re-layouts  0.61 us (3%)
    pallas_call x1, Pallas kernels, body(): pl.pallas_call(functools.partial(kernel, n, batch, block, kv, hd ** (-0.5...  22.4 us
    unnamed x1, local copies, waits for them, and re-layouts  0.61 us

profile of v3, /device:TPU:0, one launch (start us, length us, event | category | flops | bytes accessed | tf_op | source)
XLA Modules:
  0.0 23.1 jit_solution(17045003595614176702)
XLA Ops:
  0.0 22.4 %decode.1 = bf16[64,128]{1,0:T(8,128)(2,1)S(1)} custom-call(s32[16]{0:T(128)} %lengths_hbm.1, s32[8]{0:T(128)} %block_hbm.1, bf16[64,128]{1,0:T(8,128)(2,1)} %bitcast.7, bf16[8,4096,128]{2,1,0:T(8,128)(2,1)} %bitcast.5, bf16[8,4096,128]{2,1,0:T(8,128)(2,1)} %bitcast.6), custom_call_target="tpu_custom_call" | custom-call | tf_op jit(solution)/shard_map/decode/pallas_call | solution.py:291
  22.5 0.6 %copy.7 = bf16[64,1,128]{2,0,1:T(8,128)(2,1)} copy(bf16[64,1,128]{2,0,1:T(8,128)(2,1)S(1)} %bitcast.4) | data formatting | bytes 32768

commit v4 on v3

--- a/solution.py
+++ b/solution.py
@@ -11,6 +11,7 @@
 MESH_ID = pl.DeviceIdType.MESH
 LOW = -1e30
 DEAD = -3e38
+PLANE = 2
 
 
 def fold(tile, step, op):
@@ -34,7 +35,7 @@
     lengths_hbm, block_hbm, q_hbm, k_hbm, v_hbm, out_ref,
     lengths, slot_block, final, q_ref, q_all, k_buf, k_turn, v_buf, scores, sums, peaks, totals,
     best_own, best_in, tot_own, tot_in, acc_send, acc_in, mail, mail_in,
-    k_sem, v_sem, own_sem, in_sem, qs_sem, qr_sem, fs_sem, swap_sem, as_sem, ar_sem,
+    k_sem, v_sem, own_sem, in_sem, qs_sem, qr_sem, fs_sem, relay_sem, swap_sem, as_sem, ar_sem,
 ):
     slots, cols, hd = k_buf.shape
     share = q_ref.shape[0]
@@ -65,8 +66,14 @@
     q_in.start()
     peers = [(mine + r) % outer for r in range(1, outer)]
     barrier = pltpu.get_barrier_semaphore()
+    near = mine < 2 * PLANE
+    front, relaying = mine < PLANE, jnp.logical_and(mine >= PLANE, near)
+
+    def greet(o):
+        pl.semaphore_signal(barrier, inc=1, device_id={"seq": o * 2 + inner}, device_id_type=MESH_ID)
+
     for o in peers:
-        pl.semaphore_signal(barrier, inc=1, device_id={"seq": o * 2 + inner}, device_id_type=MESH_ID)
+        pl.when(jnp.logical_or(near, o >= PLANE))(functools.partial(greet, o))
     pl.semaphore_signal(barrier, inc=1, device_id={"seq": partner}, device_id_type=MESH_ID)
     len_in = pltpu.make_async_copy(lengths_hbm, lengths, in_sem.at[1])
     block_in = pltpu.make_async_copy(block_hbm, slot_block, in_sem.at[2])
@@ -104,20 +111,36 @@
             return carry
         lax.fori_loop(0, slots, one, 0)
 
-    early = mine < outer // 2
-    pl.when(early)(turn_keys)
-    pl.semaphore_wait(barrier, outer)
-
-    sends = []
+    pl.semaphore_wait(barrier, jnp.where(front, 2 * PLANE, outer))
+
+    direct = []
     for r, o in enumerate(peers):
-        sends.append(remote(q_ref, q_all.at[me], qs_sem.at[r], qr_sem.at[me], o * 2 + inner))
-    sends.append(remote(q_ref, q_all.at[me], qs_sem.at[outer - 1], qr_sem.at[me], partner))
-    for c in sends:
-        c.start()
-    pl.when(jnp.logical_not(early))(turn_keys)
+        c = remote(q_ref, q_all.at[me], qs_sem.at[r], qr_sem.at[me], o * 2 + inner)
+        direct.append((jnp.logical_or(jnp.logical_not(front), o < 2 * PLANE), c))
+    for asked, c in direct:
+        pl.when(asked)(c.start)
+    sends = [remote(q_ref, q_all.at[me], qs_sem.at[outer - 1], qr_sem.at[me], partner)]
+    sends[0].start()
+    origin = (mine + outer - PLANE) % outer * 2 + inner
+    relays = [
+        remote(q_all.at[origin], q_all.at[origin], relay_sem.at[t], qr_sem.at[origin], (2 * PLANE + t) * 2 + inner)
+        for t in range(outer - 2 * PLANE)
+    ]
+
+    def hand_on():
+        remote(q_ref, q_all.at[origin], qs_sem.at[0], qr_sem.at[origin], partner).wait_recv()
+        for c in relays:
+            c.start()
+
+    pl.when(relaying)(hand_on)
+    turn_keys()
     for r in range(1, outer):
         src = ((mine + outer - r) % outer) * 2 + inner
-        remote(q_ref, q_all.at[src], qs_sem.at[0], qr_sem.at[src], partner).wait_recv()
+        arrival = remote(q_ref, q_all.at[src], qs_sem.at[0], qr_sem.at[src], partner)
+        if r == PLANE:
+            pl.when(jnp.logical_not(relaying))(arrival.wait_recv)
+        else:
+            arrival.wait_recv()
         c = remote(q_all.at[src], q_all.at[src], fs_sem.at[r - 1], qr_sem.at[src], partner)
         c.start()
         sends.append(c)
@@ -271,6 +294,14 @@
     out_ref[...] = out.astype(jnp.bfloat16)
     for c in sends + last:
         c.wait_send()
+    for asked, c in direct:
+        pl.when(asked)(c.wait_send)
+
+    def handed_on():
+        for c in relays:
+            c.wait_send()
+
+    pl.when(relaying)(handed_on)
 
 
 def body(queries, keys, values, lengths, slot_block):
@@ -315,7 +346,7 @@
             pltpu.VMEM((outer, share + group, hd), bf16),
             pltpu.VMEM((outer, share + group, hd), bf16),
             dma((slots,)), dma((slots,)), dma, dma((3,)),
-            dma((outer,)), dma((n,)), dma((outer,)), dma((6,)),
+            dma((outer,)), dma((n,)), dma((outer,)), dma((outer,)), dma((6,)),
             dma((outer,)), dma((outer,)),
         ],
         compiler_params=pltpu.CompilerParams(

time: 23.2 us -> 22.8 us (0.983)
  Pallas kernels: 22.4 us -> 22 us
    pallas_call x1, Pallas kernels: 22.4 us -> 22 us  [body(): pl.pallas_call(functools.partial(kernel, n, batch, block, kv, hd ** (-0.5...]
where the time goes in v4:
time: 22.8 us; the launch traced here: 22.6 us
  Pallas kernels  22 us (96%)
  local copies, waits for them, and re-layouts  0.61 us (3%)
    pallas_call x1, Pallas kernels, body(): pl.pallas_call(functools.partial(kernel, n, batch, block, kv, hd ** (-0.5...  22 us
    unnamed x1, local copies, waits for them, and re-layouts  0.61 us

profile of v4, /device:TPU:0, one launch (start us, length us, event | category | flops | bytes accessed | tf_op | source)
XLA Modules:
  0.0 22.6 jit_solution(16847280004781816878)
XLA Ops:
  0.0 22.0 %decode.1 = bf16[64,128]{1,0:T(8,128)(2,1)S(1)} custom-call(s32[16]{0:T(128)} %lengths_hbm.1, s32[8]{0:T(128)} %block_hbm.1, bf16[64,128]{1,0:T(8,128)(2,1)} %bitcast.7, bf16[8,4096,128]{2,1,0:T(8,128)(2,1)} %bitcast.5, bf16[8,4096,128]{2,1,0:T(8,128)(2,1)} %bitcast.6), custom_call_target="tpu_custom_call" | custom-call | tf_op jit(solution)/shard_map/decode/pallas_call | solution.py:322
  22.0 0.6 %copy.7 = bf16[64,1,128]{2,0,1:T(8,128)(2,1)} copy(bf16[64,1,128]{2,0,1:T(8,128)(2,1)S(1)} %bitcast.4) | data formatting | bytes 32768

commit v5 on v4

--- a/solution.py
+++ b/solution.py
@@ -12,6 +12,7 @@
 LOW = -1e30
 DEAD = -3e38
 PLANE = 2
+LATE = 4
 
 
 def fold(tile, step, op):
@@ -46,8 +47,10 @@
     group = heads // kv
     held = share // group
     half = cols // 2
+    lead = slots - slots // LATE
     me = lax.axis_index("seq")
     mine, inner = me // 2, me % 2
+    other = 1 - inner
     partner = me + 1 - 2 * inner
 
     def k_copy(s):
@@ -64,16 +67,15 @@
 
     q_in = pltpu.make_async_copy(q_hbm, q_ref, in_sem.at[0])
     q_in.start()
-    peers = [(mine + r) % outer for r in range(1, outer)]
+    front, relaying = mine < PLANE, jnp.logical_and(mine >= PLANE, mine < 2 * PLANE)
+    peers = [(mine + jnp.where(relaying, outer - r, r)) % outer for r in range(1, outer)]
     barrier = pltpu.get_barrier_semaphore()
-    near = mine < 2 * PLANE
-    front, relaying = mine < PLANE, jnp.logical_and(mine >= PLANE, near)
 
     def greet(o):
-        pl.semaphore_signal(barrier, inc=1, device_id={"seq": o * 2 + inner}, device_id_type=MESH_ID)
+        pl.semaphore_signal(barrier, inc=1, device_id={"seq": o * 2 + other}, device_id_type=MESH_ID)
 
     for o in peers:
-        pl.when(jnp.logical_or(near, o >= PLANE))(functools.partial(greet, o))
+        pl.when(front | (o >= PLANE) | (o + PLANE == mine))(functools.partial(greet, o))
     pl.semaphore_signal(barrier, inc=1, device_id={"seq": partner}, device_id_type=MESH_ID)
     len_in = pltpu.make_async_copy(lengths_hbm, lengths, in_sem.at[1])
     block_in = pltpu.make_async_copy(block_hbm, slot_block, in_sem.at[2])
@@ -83,6 +85,49 @@
     own.start()
     for s in range(slots):
         k_copy(s).start()
+    for s in range(slots):
+        v_copy(s).start(priority=1)
+    q_in.wait()
+    chunk = min(half, 512)
+
+    def turn_keys():
+        def one(s, carry):
+            k_copy(s).wait()
+            for c in range(0, half, chunk):
+                k_turn[s, :hd, c : c + chunk] = k_buf[s, c : c + chunk, :].T
+                k_turn[s, hd:, c : c + chunk] = k_buf[s, half + c : half + c + chunk, :].T
+            return carry
+        lax.fori_loop(0, slots, one, 0)
+
+    pl.semaphore_wait(barrier, jnp.where(front, PLANE + 1, outer))
+
+    direct = []
+    for r, o in enumerate(peers):
+        c = remote(q_ref, q_all.at[me], qs_sem.at[r], qr_sem.at[me], o * 2 + other)
+        direct.append((jnp.logical_not(front) | (o < PLANE) | (o == mine + PLANE), c))
+    for asked, c in direct[: outer // 2]:
+        pl.when(asked)(c.start)
+    sends = [remote(q_ref, q_all.at[me], qs_sem.at[outer - 1], qr_sem.at[me], partner)]
+    sends[0].start()
+    origin = (mine + outer - PLANE) % outer * 2 + other
+    targets = [outer - 1 - t for t in range(outer - 2 * PLANE)]
+    targets += [PLANE + (mine + t) % PLANE for t in range(1, PLANE)]
+    relays = [
+        remote(q_all.at[origin], q_all.at[origin], relay_sem.at[t], qr_sem.at[origin], o * 2 + other)
+        for t, o in enumerate(targets)
+    ]
+
+    def hand_on():
+        remote(q_ref, q_all.at[origin], qs_sem.at[0], qr_sem.at[origin], partner).wait_recv()
+        for c in relays:
+            c.start()
+
+    def side(o):
+        return jnp.where(jnp.logical_not(front) & (o < PLANE) & (o + PLANE != mine), inner, other)
+
+    pl.when(relaying)(hand_on)
+    for asked, c in direct[outer // 2 :]:
+        pl.when(asked)(c.start)
     sums[...] = jnp.zeros_like(sums)
     len_in.wait()
     block_in.wait()
@@ -98,44 +143,10 @@
         for s in range(slots):
             last = jnp.where(seqs[s] == b, s, last)
         final[b] = last
-    q_in.wait()
-    chunk = min(half, 512)
-
-    def turn_keys():
-        def one(s, carry):
-            k_copy(s).wait()
-            v_copy(s).start()
-            for c in range(0, half, chunk):
-                k_turn[s, :hd, c : c + chunk] = k_buf[s, c : c + chunk, :].T
-                k_turn[s, hd:, c : c + chunk] = k_buf[s, half + c : half + c + chunk, :].T
-            return carry
-        lax.fori_loop(0, slots, one, 0)
-
-    pl.semaphore_wait(barrier, jnp.where(front, 2 * PLANE, outer))
-
-    direct = []
-    for r, o in enumerate(peers):
-        c = remote(q_ref, q_all.at[me], qs_sem.at[r], qr_sem.at[me], o * 2 + inner)
-        direct.append((jnp.logical_or(jnp.logical_not(front), o < 2 * PLANE), c))
-    for asked, c in direct:
-        pl.when(asked)(c.start)
-    sends = [remote(q_ref, q_all.at[me], qs_sem.at[outer - 1], qr_sem.at[me], partner)]
-    sends[0].start()
-    origin = (mine + outer - PLANE) % outer * 2 + inner
-    relays = [
-        remote(q_all.at[origin], q_all.at[origin], relay_sem.at[t], qr_sem.at[origin], (2 * PLANE + t) * 2 + inner)
-        for t in range(outer - 2 * PLANE)
-    ]
-
-    def hand_on():
-        remote(q_ref, q_all.at[origin], qs_sem.at[0], qr_sem.at[origin], partner).wait_recv()
-        for c in relays:
-            c.start()
-
-    pl.when(relaying)(hand_on)
     turn_keys()
     for r in range(1, outer):
-        src = ((mine + outer - r) % outer) * 2 + inner
+        o = (mine + outer - r) % outer
+        src = o * 2 + side(o)
         arrival = remote(q_ref, q_all.at[src], qs_sem.at[0], qr_sem.at[src], partner)
         if r == PLANE:
             pl.when(jnp.logical_not(relaying))(arrival.wait_recv)
@@ -147,7 +158,8 @@
     own.wait()
     remote(q_ref, q_all.at[partner], qs_sem.at[0], qr_sem.at[partner], partner).wait_recv()
     for r in range(1, outer):
-        src = ((mine + outer - r) % outer) * 2 + 1 - inner
+        o = (mine + outer - r) % outer
+        src = o * 2 + 1 - side(o)
         remote(q_ref, q_all.at[src], qs_sem.at[0], qr_sem.at[src], partner).wait_recv()
 
     lane = lax.broadcasted_iota(jnp.int32, (group, LANES), 1)
@@ -203,13 +215,13 @@
         sums[s] = out[:heads, :hd] + out[heads:, hd:]
         totals[s] = fold(total, kv, jnp.add)
 
-    def loop(step):
+    def loop(step, end):
         def one(s, carry):
             step(s)
             return carry
-        lax.fori_loop(0, slots, one, 0, unroll=True)
-
-    loop(score)
+        lax.fori_loop(0, end, one, 0, unroll=True)
+
+    loop(score, slots)
     best = jnp.full((group, LANES), LOW, jnp.float32)
     for s in range(slots):
         best = jnp.maximum(best, jnp.where(home == seqs[s], peaks[s], LOW))
@@ -218,15 +230,26 @@
     swap.start()
     for s in range(slots):
         v_copy(s).wait()
-    loop(weigh)
+    loop(weigh, lead)
     swap.wait()
     best = jnp.maximum(best_own[...], best_in[...])
-    total = jnp.zeros((group, LANES), jnp.float32)
-    for s in range(slots):
+
+    def gather(s, total):
         ours = fold(jnp.where(home == seqs[s], best, LOW), kv, jnp.maximum)
         scale = jnp.exp2(peaks[s] - ours)
-        total = total + jnp.where(home == seqs[s], totals[s] * scale, 0.0)
         sums[s] = sums[s] * spread(scale, 0, kv) + sums[before[s]]
+        return total + jnp.where(home == seqs[s], totals[s] * scale, 0.0)
+
+    total = jnp.zeros((group, LANES), jnp.float32)
+    done = 0
+    for s in range(lead, slots):
+        weigh(s)
+        upto = lead * (s + 1 - lead) // (slots - lead)
+        for t in range(done, upto):
+            total = gather(t, total)
+        done = upto
+    for t in range(done, slots):
+        total = gather(t, total)
 
     def piece(o, core):
         j = o * 2 + core
@@ -238,7 +261,7 @@
     diagonal = lane % (LANES // 2) // kv == sub
     tot_own[...] = total
     for o in range(outer):
-        acc_send[o] = piece(o, 1 - inner).astype(jnp.bfloat16)
+        acc_send[o] = piece(o, inner).astype(jnp.bfloat16)
     c1 = remote(acc_send, acc_in, swap_sem.at[2], swap_sem.at[3], partner)
     c2 = remote(tot_own, tot_in, swap_sem.at[4], swap_sem.at[5], partner)
     c2.start()
@@ -248,7 +271,7 @@
     stats = []
     for r in range(1, outer + 1):
         o = (mine + r) % outer
-        j = o * 2 + inner
+        j = o * 2 + other
         tb = fold(jnp.where(home == j // per, best, LOW), kv, jnp.maximum)
         tt = fold(jnp.where(home == j // per, total, 0.0), kv, jnp.add)
         if per > 1:
@@ -264,16 +287,13 @@
     last = []
     for r in range(1, outer + 1):
         o = (mine + r) % outer
-        both = (piece(o, inner) + acc_in[o].astype(jnp.float32)).astype(jnp.bfloat16)
-        into = mail_in if r == outer else mail
-        into[o, :share] = both
-        into[o, share:] = stats[r - 1]
-        if r < outer:
-            c = remote(mail.at[o], mail_in.at[mine], as_sem.at[r - 1], ar_sem.at[mine], o * 2 + inner)
-            c.start()
-            last.append(c)
-    for r in range(1, outer):
-        o = (mine + outer - r) % outer
+        both = (piece(o, other) + acc_in[o].astype(jnp.float32)).astype(jnp.bfloat16)
+        mail[o, :share] = both
+        mail[o, share:] = stats[r - 1]
+        c = remote(mail.at[o], mail_in.at[mine], as_sem.at[r - 1], ar_sem.at[mine], o * 2 + other)
+        c.start()
+        last.append(c)
+    for o in range(outer):
         remote(mail.at[o], mail_in.at[o], as_sem.at[0], ar_sem.at[o], partner).wait_recv()
     tops = []
     for o in range(outer):

time: 22.8 us -> 22.1 us (0.969)
  Pallas kernels: 22 us -> 21.2 us
    pallas_call x1, Pallas kernels: 22 us -> 21.2 us  [body(): pl.pallas_call(functools.partial(kernel, n, batch, block, kv, hd ** (-0.5...]
where the time goes in v5:
time: 22.1 us; the launch traced here: 21.8 us
  Pallas kernels  21.2 us (96%)
  local copies, waits for them, and re-layouts  0.61 us (3%)
    pallas_call x1, Pallas kernels, body(): pl.pallas_call(functools.partial(kernel, n, batch, block, kv, hd ** (-0.5...  21.2 us
    unnamed x1, local copies, waits for them, and re-layouts  0.61 us

profile of v5, /device:TPU:0, one launch (start us, length us, event | category | flops | bytes accessed | tf_op | source)
XLA Modules:
  0.0 21.8 jit_solution(15760419268601899042)
XLA Ops:
  0.0 21.2 %decode.1 = bf16[64,128]{1,0:T(8,128)(2,1)S(1)} custom-call(s32[16]{0:T(128)} %lengths_hbm.1, s32[8]{0:T(128)} %block_hbm.1, bf16[64,128]{1,0:T(8,128)(2,1)} %bitcast.7, bf16[8,4096,128]{2,1,0:T(8,128)(2,1)} %bitcast.5, bf16[8,4096,128]{2,1,0:T(8,128)(2,1)} %bitcast.6), custom_call_target="tpu_custom_call" | custom-call | tf_op jit(solution)/shard_map/decode/pallas_call | solution.py:342
  21.2 0.6 %copy.7 = bf16[64,1,128]{2,0,1:T(8,128)(2,1)} copy(bf16[64,1,128]{2,0,1:T(8,128)(2,1)S(1)} %bitcast.4) | data formatting | bytes 32768

commit v6 on v5

--- a/solution.py
+++ b/solution.py
@@ -36,7 +36,7 @@
     lengths_hbm, block_hbm, q_hbm, k_hbm, v_hbm, out_ref,
     lengths, slot_block, final, q_ref, q_all, k_buf, k_turn, v_buf, scores, sums, peaks, totals,
     best_own, best_in, tot_own, tot_in, acc_send, acc_in, mail, mail_in,
-    k_sem, v_sem, own_sem, in_sem, qs_sem, qr_sem, fs_sem, relay_sem, swap_sem, as_sem, ar_sem,
+    k_sem, v_sem, own_sem, in_sem, qs_sem, qr_sem, fs_sem, relay_sem, ready, swap_sem, as_sem, ar_sem,
 ):
     slots, cols, hd = k_buf.shape
     share = q_ref.shape[0]
@@ -67,6 +67,8 @@
 
     q_in = pltpu.make_async_copy(q_hbm, q_ref, in_sem.at[0])
     q_in.start()
+    edge = outer - PLANE
+    late = mine >= edge
     front, relaying = mine < PLANE, jnp.logical_and(mine >= PLANE, mine < 2 * PLANE)
     peers = [(mine + jnp.where(relaying, outer - r, r)) % outer for r in range(1, outer)]
     barrier = pltpu.get_barrier_semaphore()
@@ -75,7 +77,8 @@
         pl.semaphore_signal(barrier, inc=1, device_id={"seq": o * 2 + other}, device_id_type=MESH_ID)
 
     for o in peers:
-        pl.when(front | (o >= PLANE) | (o + PLANE == mine))(functools.partial(greet, o))
+        asks = jnp.where(late, o >= edge, front | (o >= PLANE) | (o + PLANE == mine))
+        pl.when(asks)(functools.partial(greet, o))
     pl.semaphore_signal(barrier, inc=1, device_id={"seq": partner}, device_id_type=MESH_ID)
     len_in = pltpu.make_async_copy(lengths_hbm, lengths, in_sem.at[1])
     block_in = pltpu.make_async_copy(block_hbm, slot_block, in_sem.at[2])
@@ -99,35 +102,57 @@
             return carry
         lax.fori_loop(0, slots, one, 0)
 
-    pl.semaphore_wait(barrier, jnp.where(front, PLANE + 1, outer))
-
+    pl.semaphore_wait(barrier, jnp.where(front, PLANE + 1, jnp.where(late, outer, edge)))
+
+    def announce():
+        for o in range(PLANE, edge):
+            pl.semaphore_signal(ready, inc=1, device_id={"seq": o * 2 + other}, device_id_type=MESH_ID)
+
+    pl.when(late)(announce)
     direct = []
     for r, o in enumerate(peers):
         c = remote(q_ref, q_all.at[me], qs_sem.at[r], qr_sem.at[me], o * 2 + other)
-        direct.append((jnp.logical_not(front) | (o < PLANE) | (o == mine + PLANE), c))
-    for asked, c in direct[: outer // 2]:
-        pl.when(asked)(c.start)
+        asked = jnp.logical_not(front) | (o < PLANE) | (o == mine + PLANE)
+        direct.append((asked, late | (o < edge), c))
+    for asked, soon, c in direct:
+        pl.when(asked & soon)(c.start)
     sends = [remote(q_ref, q_all.at[me], qs_sem.at[outer - 1], qr_sem.at[me], partner)]
     sends[0].start()
     origin = (mine + outer - PLANE) % outer * 2 + other
-    targets = [outer - 1 - t for t in range(outer - 2 * PLANE)]
+    targets = [edge + t for t in range(PLANE)]
     targets += [PLANE + (mine + t) % PLANE for t in range(1, PLANE)]
+    targets += [edge - 1 - t for t in range(edge - 2 * PLANE)]
     relays = [
         remote(q_all.at[origin], q_all.at[origin], relay_sem.at[t], qr_sem.at[origin], o * 2 + other)
         for t, o in enumerate(targets)
     ]
 
+    def receive_first():
+        remote(q_ref, q_all.at[origin], qs_sem.at[0], qr_sem.at[origin], partner).wait_recv()
+        for c in relays[PLANE : 2 * PLANE - 1]:
+            c.start()
+
     def hand_on():
-        remote(q_ref, q_all.at[origin], qs_sem.at[0], qr_sem.at[origin], partner).wait_recv()
-        for c in relays:
+        for c in relays[:PLANE]:
+            c.start()
+
+    def hand_back():
+        for c in relays[2 * PLANE - 1 :]:
             c.start()
 
     def side(o):
         return jnp.where(jnp.logical_not(front) & (o < PLANE) & (o + PLANE != mine), inner, other)
 
+    pl.when(relaying)(receive_first)
+
+    def wait_late():
+        pl.semaphore_wait(ready, PLANE)
+
+    pl.when(relaying)(hand_back)
+    pl.when(jnp.logical_not(front | late))(wait_late)
     pl.when(relaying)(hand_on)
-    for asked, c in direct[outer // 2 :]:
-        pl.when(asked)(c.start)
+    for asked, soon, c in direct:
+        pl.when(asked & jnp.logical_not(soon))(c.start)
     sums[...] = jnp.zeros_like(sums)
     len_in.wait()
     block_in.wait()
@@ -314,7 +339,7 @@
     out_ref[...] = out.astype(jnp.bfloat16)
     for c in sends + last:
         c.wait_send()
-    for asked, c in direct:
+    for asked, _, c in direct:
         pl.when(asked)(c.wait_send)
 
     def handed_on():
@@ -366,7 +391,7 @@
             pltpu.VMEM((outer, share + group, hd), bf16),
             pltpu.VMEM((outer, share + group, hd), bf16),
             dma((slots,)), dma((slots,)), dma, dma((3,)),
-            dma((outer,)), dma((n,)), dma((outer,)), dma((outer,)), dma((6,)),
+            dma((outer,)), dma((n,)), dma((outer,)), dma((outer,)), pltpu.SemaphoreType.REGULAR, dma((6,)),
             dma((outer,)), dma((outer,)),
         ],
         compiler_params=pltpu.CompilerParams(

time: 22.1 us -> 21.3 us (0.964)
  Pallas kernels: 21.2 us -> 20.4 us
    pallas_call x1, Pallas kernels: 21.2 us -> 20.4 us  [body(): pl.pallas_call(functools.partial(kernel, n, batch, block, kv, hd ** (-0.5...]
where the time goes in v6:
time: 21.3 us; the launch traced here: 21 us
  Pallas kernels  20.4 us (96%)
  local copies, waits for them, and re-layouts  0.61 us (3%)
    pallas_call x1, Pallas kernels, body(): pl.pallas_call(functools.partial(kernel, n, batch, block, kv, hd ** (-0.5...  20.4 us
    unnamed x1, local copies, waits for them, and re-layouts  0.61 us

profile of v6, /device:TPU:0, one launch (start us, length us, event | category | flops | bytes accessed | tf_op | source)
XLA Modules:
  0.0 21.0 jit_solution(3801538846440450454)
XLA Ops:
  0.0 20.4 %decode.1 = bf16[64,128]{1,0:T(8,128)(2,1)S(1)} custom-call(s32[16]{0:T(128)} %lengths_hbm.1, s32[8]{0:T(128)} %block_hbm.1, bf16[64,128]{1,0:T(8,128)(2,1)} %bitcast.7, bf16[8,4096,128]{2,1,0:T(8,128)(2,1)} %bitcast.5, bf16[8,4096,128]{2,1,0:T(8,128)(2,1)} %bitcast.6), custom_call_target="tpu_custom_call" | custom-call | tf_op jit(solution)/shard_map/decode/pallas_call | solution.py:367
  20.4 0.6 %copy.7 = bf16[64,1,128]{2,0,1:T(8,128)(2,1)} copy(bf16[64,1,128]{2,0,1:T(8,128)(2,1)S(1)} %bitcast.4) | data formatting | bytes 32768

commit v7 on v6

--- a/solution.py
+++ b/solution.py
@@ -91,7 +91,7 @@
     for s in range(slots):
         v_copy(s).start(priority=1)
     q_in.wait()
-    chunk = min(half, 512)
+    chunk = min(half, 256)
 
     def turn_keys():
         def one(s, carry):
@@ -119,7 +119,7 @@
     sends = [remote(q_ref, q_all.at[me], qs_sem.at[outer - 1], qr_sem.at[me], partner)]
     sends[0].start()
     origin = (mine + outer - PLANE) % outer * 2 + other
-    targets = [edge + t for t in range(PLANE)]
+    targets = [outer - 1 - t for t in range(PLANE)]
     targets += [PLANE + (mine + t) % PLANE for t in range(1, PLANE)]
     targets += [edge - 1 - t for t in range(edge - 2 * PLANE)]
     relays = [
@@ -240,22 +240,23 @@
         sums[s] = out[:heads, :hd] + out[heads:, hd:]
         totals[s] = fold(total, kv, jnp.add)
 
-    def loop(step, end):
+    def loop(step, start, end):
         def one(s, carry):
             step(s)
             return carry
-        lax.fori_loop(0, end, one, 0, unroll=True)
-
-    loop(score, slots)
+        lax.fori_loop(start, end, one, 0, unroll=True)
+
+    for s in range(slots):
+        v_copy(s).wait()
+    loop(score, 0, slots)
     best = jnp.full((group, LANES), LOW, jnp.float32)
     for s in range(slots):
         best = jnp.maximum(best, jnp.where(home == seqs[s], peaks[s], LOW))
     best_own[...] = best
     swap = remote(best_own, best_in, swap_sem.at[0], swap_sem.at[1], partner)
+    weigh(0)
     swap.start()
-    for s in range(slots):
-        v_copy(s).wait()
-    loop(weigh, lead)
+    loop(weigh, 1, lead)
     swap.wait()
     best = jnp.maximum(best_own[...], best_in[...])
 
@@ -285,12 +286,16 @@
     sub = lax.broadcasted_iota(jnp.int32, (group, LANES), 0)
     diagonal = lane % (LANES // 2) // kv == sub
     tot_own[...] = total
-    for o in range(outer):
-        acc_send[o] = piece(o, inner).astype(jnp.bfloat16)
-    c1 = remote(acc_send, acc_in, swap_sem.at[2], swap_sem.at[3], partner)
-    c2 = remote(tot_own, tot_in, swap_sem.at[4], swap_sem.at[5], partner)
+    c2 = remote(tot_own, tot_in, swap_sem.at[2], swap_sem.at[3], partner)
     c2.start()
-    c1.start()
+    shares = []
+    for h in range(2):
+        at = pl.ds(h * (outer // 2), outer // 2)
+        for r in range(h * (outer // 2), (h + 1) * (outer // 2)):
+            acc_send[r] = piece((mine + r + 1) % outer, inner).astype(jnp.bfloat16)
+        c = remote(acc_send.at[at], acc_in.at[at], swap_sem.at[4 + h], swap_sem.at[6 + h], partner)
+        c.start()
+        shares.append(c)
     c2.wait()
     total = tot_own[...] + tot_in[...]
     stats = []
@@ -308,11 +313,12 @@
         second = (line - first).astype(jnp.bfloat16).astype(jnp.float32)
         third = line - first - second
         stats.append(jnp.where(sub == 0, first, jnp.where(sub == 1, second, third)).astype(jnp.bfloat16))
-    c1.wait()
     last = []
     for r in range(1, outer + 1):
         o = (mine + r) % outer
-        both = (piece(o, other) + acc_in[o].astype(jnp.float32)).astype(jnp.bfloat16)
+        if (r - 1) % (outer // 2) == 0:
+            shares[(r - 1) // (outer // 2)].wait()
+        both = (piece(o, other) + acc_in[r - 1].astype(jnp.float32)).astype(jnp.bfloat16)
         mail[o, :share] = both
         mail[o, share:] = stats[r - 1]
         c = remote(mail.at[o], mail_in.at[mine], as_sem.at[r - 1], ar_sem.at[mine], o * 2 + other)
@@ -391,7 +397,7 @@
             pltpu.VMEM((outer, share + group, hd), bf16),
             pltpu.VMEM((outer, share + group, hd), bf16),
             dma((slots,)), dma((slots,)), dma, dma((3,)),
-            dma((outer,)), dma((n,)), dma((outer,)), dma((outer,)), pltpu.SemaphoreType.REGULAR, dma((6,)),
+            dma((outer,)), dma((n,)), dma((outer,)), dma((outer,)), pltpu.SemaphoreType.REGULAR, dma((8,)),
             dma((outer,)), dma((outer,)),
         ],
         compiler_params=pltpu.CompilerParams(

time: 21.3 us -> 21.3 us (level)
  no operation moved by 1% of the time
where the time goes in v7:
time: 21.3 us; the launch traced here: 21 us
  Pallas kernels  20.4 us (96%)
  local copies, waits for them, and re-layouts  0.61 us (3%)
    pallas_call x1, Pallas kernels, body(): pl.pallas_call(functools.partial(kernel, n, batch, block, kv, hd ** (-0.5...  20.4 us
    unnamed x1, local copies, waits for them, and re-layouts  0.61 us

profile of v7, /device:TPU:0, one launch (start us, length us, event | category | flops | bytes accessed | tf_op | source)
XLA Modules:
  0.0 21.0 jit_solution(3839688189841043587)
XLA Ops:
  0.0 20.4 %decode.1 = bf16[64,128]{1,0:T(8,128)(2,1)S(1)} custom-call(s32[16]{0:T(128)} %lengths_hbm.1, s32[8]{0:T(128)} %block_hbm.1, bf16[64,128]{1,0:T(8,128)(2,1)} %bitcast.7, bf16[8,4096,128]{2,1,0:T(8,128)(2,1)} %bitcast.5, bf16[8,4096,128]{2,1,0:T(8,128)(2,1)} %bitcast.6), custom_call_target="tpu_custom_call" | custom-call | tf_op jit(solution)/shard_map/decode/pallas_call | solution.py:373
  20.4 0.6 %copy.7 = bf16[64,1,128]{2,0,1:T(8,128)(2,1)} copy(bf16[64,1,128]{2,0,1:T(8,128)(2,1)S(1)} %bitcast.4) | data formatting | bytes 32768

commit v8 on v7

--- a/solution.py
+++ b/solution.py
@@ -12,7 +12,7 @@
 LOW = -1e30
 DEAD = -3e38
 PLANE = 2
-LATE = 4
+LATE = 8
 
 
 def fold(tile, step, op):

time: 21.3 us -> 21.2 us (level)
  no operation moved by 1% of the time
where the time goes in v8:
time: 21.2 us; the launch traced here: 21 us
  Pallas kernels  20.3 us (96%)
  local copies, waits for them, and re-layouts  0.61 us (3%)
    pallas_call x1, Pallas kernels, body(): pl.pallas_call(functools.partial(kernel, n, batch, block, kv, hd ** (-0.5...  20.3 us
    unnamed x1, local copies, waits for them, and re-layouts  0.61 us

profile of v8, /device:TPU:0, one launch (start us, length us, event | category | flops | bytes accessed | tf_op | source)
XLA Modules:
  0.0 21.0 jit_solution(1498025533189172433)
XLA Ops:
  0.0 20.3 %decode.1 = bf16[64,128]{1,0:T(8,128)(2,1)S(1)} custom-call(s32[16]{0:T(128)} %lengths_hbm.1, s32[8]{0:T(128)} %block_hbm.1, bf16[64,128]{1,0:T(8,128)(2,1)} %bitcast.7, bf16[8,4096,128]{2,1,0:T(8,128)(2,1)} %bitcast.5, bf16[8,4096,128]{2,1,0:T(8,128)(2,1)} %bitcast.6), custom_call_target="tpu_custom_call" | custom-call | tf_op jit(solution)/shard_map/decode/pallas_call | solution.py:373
  20.4 0.6 %copy.7 = bf16[64,1,128]{2,0,1:T(8,128)(2,1)} copy(bf16[64,1,128]{2,0,1:T(8,128)(2,1)S(1)} %bitcast.4) | data formatting | bytes 32768
